TPU v7x, 32 devices: a whole 2x2x4 slice. The times are simulated.
32 devices in a mesh: groups: 2 (over y), dp: 4 (over z), rep: 4 (over x, core).
Axes of the slice: x: 2, y: 2, z: 4, core: 2. Of those that a mesh axis runs over, the one named last changes fastest.
Arguments:
- latent_store: bfloat16 [8, 48, 576, 128], P(('groups', 'dp'), 'rep'), parts along dimension 0, may hold values from -6 to 6
- page_rank: int32 [8, 48], P('groups', 'rep'), parts along dimension 0, may hold values from 0 to 3, as said below
- page_index: int32 [8, 48], P('groups', 'rep'), parts along dimension 0, may hold values from 0 to 11, as said below
- lengths: int32 [8, 1], P('groups'), parts along dimension 0, may hold values from 1536 to 6144, as said below
- queries: bfloat16 [16, 36864], P(('groups', 'dp')), parts along dimension 0, may hold values from -250 to 250
- new_latent: bfloat16 [16, 576], P(('groups', 'dp')), parts along dimension 0, may hold values from -4 to 4
- up_value: bfloat16 [64, 512, 128], P('dp'), may hold values from -0.25 to 0.25
- out_proj: bfloat16 [8192, 7168], P('dp', 'rep'), may hold values from -0.0625 to 0.0625
- residual: bfloat16 [16, 7168], P(('groups', 'dp'), 'rep'), parts along dimension 0, may hold values from -11 to 11
- norm_gain: float32 [7168], P('rep'), may hold values from 0.1 to 1.9
- w_gate: bfloat16 [7168, 12288], P('rep', 'dp'), may hold values from -0.0625 to 0.0625
- w_up: bfloat16 [7168, 12288], P('rep', 'dp'), may hold values from -0.0625 to 0.0625
- w_down: bfloat16 [12288, 7168], P('dp', 'rep'), may hold values from -0.0546875 to 0.0546875
Outputs:
- layer_out: bfloat16 [16, 7168], P(('groups', 'dp'), 'rep'), parts along dimension 0
There are 2 independent parts, one for each index of `groups`. A program takes and returns all parts, laid end to end along the dimension named above; an argument that names none is the same for every part. Nothing has to cross between parts.
Inputs may be any that keep to these rules, and one draw needn't show every extreme that they name: page_rank[d, q] is the storage rank holding slot q of rank d, on its device with rep index q // 12; one storage device holds at most 3 slot of one rank, and some holds exactly 3. page_index[d, q] is the slot's page among the 12 pages of its storage device; over all ranks every page of every storage device is named by exactly one slot. `lengths`: some request has exactly 6144 tokens.
All inputs are finite; a program needn't handle non-finite values.
Results may differ from a plain program's by a relative error of at most 0.015.
Values may be sent and summed in bfloat16 or wider, within the bound.
A program may use at most 128 MiB of HBM per device.

v0:
```python
import math

import jax
import jax.numpy as jnp
from jax import lax
from jax.sharding import PartitionSpec as P

D = 7168
CKV = 512
PAGE = 128
PAGES = 48


score_scale = 1.0 / math.sqrt(192.0)
epsilon = 1e-06
mask_value = -1e30


def merged_2(array, axis, join):
    gathered = jax.tree.map(
        lambda a, kind: lax.all_gather(a.astype(kind), axis),
        array,
        jax.tree.map(lambda a: jnp.bfloat16 if a.dtype == jnp.float32 else a.dtype, array),
    )

    def take(source):
        return jax.tree.map(
            lambda a, own: lax.dynamic_index_in_dim(a, source, 0, False).astype(own.dtype),
            gathered,
            array,
        )

    return lax.fori_loop(
        1, lax.axis_size(axis), lambda source, state: join(state, take(source)), take(0)
    )


def page_partials(page_keys, page_queries, key_counts):
    scores = (
        jnp.einsum("pshl,plt->psht", page_queries, page_keys, preferred_element_type=jnp.float32)
        * score_scale
    )
    places = lax.broadcasted_iota(jnp.int32, scores.shape, 3)
    visible = places < key_counts[:, None, None, None]
    scores = jnp.where(visible, scores, mask_value)
    row_peak = jnp.max(scores, axis=3)
    weights = jnp.where(visible, jnp.exp(scores - row_peak[..., None]), 0.0)
    row_total = jnp.sum(weights, axis=3)
    partial_value = jnp.einsum(
        "psht,pct->pshc",
        weights.astype(jnp.bfloat16),
        page_keys[:, :CKV, :],
        preferred_element_type=jnp.float32,
    )
    return (partial_value, row_peak, row_total)


def join_pages(partial_value, row_peak, row_total, slot_request, requests):
    owner_mask = slot_request[None, :] == jnp.arange(requests, dtype=jnp.int32)[:, None]
    spread = owner_mask[:, :, None, None]
    best_peak = jnp.max(jnp.where(spread, row_peak[None], mask_value), axis=1)
    factor = jnp.where(spread, jnp.exp(row_peak[None] - best_peak[:, None]), 0.0)
    joined = jnp.einsum("jpsh,pshc->jshc", factor, partial_value, precision=lax.Precision.HIGHEST)
    summed = jnp.sum(factor * row_total[None], axis=1)
    return (joined, best_peak, summed)


def combine(former, latter):
    former_sum, former_peak, former_total = former
    latter_sum, latter_peak, latter_total = latter
    highest = jnp.maximum(former_peak, latter_peak)
    former_scale = jnp.exp(former_peak - highest)
    latter_scale = jnp.exp(latter_peak - highest)
    merged_sum = former_sum * former_scale[..., None] + latter_sum * latter_scale[..., None]
    return (merged_sum, highest, former_total * former_scale + latter_total * latter_scale)


def fresh_partial(query_rows, fresh_rows, active):
    scores = (
        jnp.einsum("jshl,jul->jshu", query_rows, fresh_rows, preferred_element_type=jnp.float32)
        * score_scale
    )
    step_query = lax.broadcasted_iota(jnp.int32, scores.shape, 1)
    step_key = lax.broadcasted_iota(jnp.int32, scores.shape, 3)
    visible = (step_key <= step_query) & active
    scores = jnp.where(visible, scores, mask_value)
    row_peak = jnp.max(scores, axis=3)
    weights = jnp.where(visible, jnp.exp(scores - row_peak[..., None]), 0.0)
    row_total = jnp.sum(weights, axis=3)
    partial_value = jnp.einsum(
        "jshu,juc->jshc",
        weights.astype(jnp.bfloat16),
        fresh_rows[:, :, :CKV],
        preferred_element_type=jnp.float32,
    )
    return (partial_value, row_peak, row_total)


def on_device(
    latent_store,
    page_rank,
    page_index,
    lengths,
    queries,
    new_latent,
    up_value,
    out_proj,
    residual,
    norm_gain,
    w_gate,
    w_up,
    w_down,
):
    my_rank = lax.axis_index("dp")
    my_column = lax.axis_index("rep")
    rank_count, slot_count = page_rank.shape
    capacity = (slot_count + rank_count - 1) // rank_count
    requests = lengths.shape[1]
    rows_here = residual.shape[0]
    steps_count = rows_here // requests
    latent_width = new_latent.shape[1]
    head_count = queries.shape[1] // latent_width
    query_rows = queries.reshape(requests, steps_count, head_count, latent_width)
    fresh_rows = new_latent.reshape(requests, steps_count, latent_width)
    slot_order = jnp.arange(slot_count, dtype=jnp.int32)
    request_ids = jnp.arange(requests, dtype=jnp.int32)
    cap_ids = jnp.arange(capacity, dtype=jnp.int32)
    global_slot = my_column * slot_count + slot_order
    slot_request = global_slot // PAGES
    slot_page = global_slot % PAGES
    own_lengths = lax.dynamic_index_in_dim(lengths, my_rank, 0, keepdims=False)
    slot_length = jnp.sum(
        jnp.where(slot_request[:, None] == request_ids[None, :], own_lengths[None, :], 0), axis=1
    )
    key_counts = jnp.clip(slot_length - slot_page * PAGE, 0, PAGE)
    my_sources = lax.dynamic_index_in_dim(page_rank, my_rank, 0, keepdims=False)
    earlier = (my_sources[None, :] == my_sources[:, None]) & (
        slot_order[None, :] < slot_order[:, None]
    )
    arrival_rank = jnp.sum(earlier.astype(jnp.int32), axis=1)
    arrival_slot = my_sources * capacity + arrival_rank
    held_here = page_rank == my_rank
    held_order = jnp.cumsum(held_here.astype(jnp.int32), axis=1) - 1
    selector = held_here[:, None, :] & (held_order[:, None, :] == cap_ids[None, :, None])
    sent_valid = jnp.any(selector, axis=2).reshape(-1)
    sent_page = jnp.sum(jnp.where(selector, page_index[:, None, :], 0), axis=2).reshape(-1)
    stored = latent_store[0]
    outgoing = jnp.take(stored, sent_page, axis=0)
    outgoing = jnp.where(sent_valid[:, None, None], outgoing, jnp.zeros_like(outgoing))
    arrived = lax.all_to_all(outgoing, "dp", split_axis=0, concat_axis=0, tiled=True)
    restored = jnp.take(arrived, arrival_slot, axis=0)
    page_queries = jnp.take(query_rows, slot_request, axis=0)
    partial_value, row_peak, row_total = page_partials(restored, page_queries, key_counts)
    joined = join_pages(partial_value, row_peak, row_total, slot_request, requests)
    local_part = combine(joined, fresh_partial(query_rows, fresh_rows, my_column == 0))
    merged = merged_2(local_part, "rep", combine)
    attention = (
        (merged[0] / merged[2][..., None]).astype(jnp.bfloat16).reshape(rows_here, head_count, CKV)
    )
    headed = lax.all_to_all(attention, "dp", split_axis=1, concat_axis=0, tiled=True)
    values = jnp.einsum("rhc,hcv->rhv", headed, up_value, preferred_element_type=jnp.float32)
    values = values.astype(jnp.bfloat16).reshape(headed.shape[0], -1)
    picked = values
    attn_out = lax.psum_scatter(
        jnp.dot(picked, out_proj, preferred_element_type=jnp.float32).astype(jnp.bfloat16),
        "dp",
        scatter_dimension=0,
        tiled=True,
    ).astype(jnp.float32)
    mixed_rows = residual.astype(jnp.float32) + attn_out
    squares = lax.psum(jnp.sum(mixed_rows * mixed_rows, axis=1), "rep")
    normed = (mixed_rows * lax.rsqrt(squares / D + epsilon)[:, None] * norm_gain).astype(
        jnp.bfloat16
    )
    piece = lax.all_gather(normed, "dp", axis=0, tiled=True)
    gate_part = jnp.dot(piece, w_gate, preferred_element_type=jnp.float32)
    up_part = jnp.dot(piece, w_up, preferred_element_type=jnp.float32)
    partial_rows = jnp.concatenate([gate_part, up_part], axis=1)
    gate_up = lax.psum(partial_rows.astype(jnp.bfloat16), "rep").astype(jnp.float32)
    hidden_width = w_gate.shape[1]
    hidden = (jax.nn.silu(gate_up[:, :hidden_width]) * gate_up[:, hidden_width:]).astype(
        jnp.bfloat16
    )
    picked = hidden
    mlp_out = lax.psum_scatter(
        jnp.dot(picked, w_down, preferred_element_type=jnp.float32).astype(jnp.bfloat16),
        "dp",
        scatter_dimension=0,
        tiled=True,
    ).astype(jnp.float32)
    return (mixed_rows + mlp_out).astype(jnp.bfloat16)


def solution(mesh):
    in_specs = (
        P(("groups", "dp"), "rep", None, None),
        P("groups", "rep"),
        P("groups", "rep"),
        P("groups", None),
        P(("groups", "dp"), None),
        P(("groups", "dp"), None),
        P("dp", None, None),
        P("dp", "rep"),
        P(("groups", "dp"), "rep"),
        P("rep"),
        P("rep", "dp"),
        P("rep", "dp"),
        P("dp", "rep"),
    )
    out_specs = P(("groups", "dp"), "rep")
    return jax.shard_map(
        on_device, mesh=mesh, in_specs=in_specs, out_specs=out_specs, check_vma=False
    )
```

profile of v0, /device:TPU:0, one launch (start us, length us, event | category | flops | bytes accessed | tf_op | source)
XLA Modules:
  0.0 225.6 jit_solution(1305932446610789168)
XLA Ops:
  6.5 0.8 fusion.66
  7.4 0.2 reduce_window_sum.11
  7.6 0.1 fusion.45
  7.7 0.8 select_reduce_fusion.1
  8.5 0.1 copy.21
  8.8 0.1 copy.20
  9.0 3.5 %gather_fusion = bf16[12,576,128]{2,1,0:T(8,128)(2,1)} fusion(bf16[12,576,128]{2,1,0:T(8,128)(2,1)} %bitcast.145, s32[1024]{0:T(1024)S(1)} %pad_clamp_fusion.1), kind=kCustom, calls=%fused_computation.clone | custom fusion | bytes 3538992 | tf_op jit(solution)/shard_map/jit(_take)/gather | solution.py:148
  12.5 2.9 %select_select_fusion = bf16[12,576,128]{2,1,0:T(8,128)(2,1)} fusion(bf16[12,576,128]{2,1,0:T(8,128)(2,1)} %gather_fusion, pred[12]{0:T(512)(128)(4,1)S(1)} %get-tuple-element.237, pred[12]{0:T(512)(128)(4,1)S(1)} %broadcast_in_dim.122), kind=kLoop, calls=%fused_computation.26 | loop fusion | flops 1769472 | bytes 3538968 | tf_op jit(solution)/shard_map/jit(_where)/select_n | solution.py:149
  15.4 6.5 %all-to-all-start = ((bf16[12,576,128]{2,1,0:T(8,128)(2,1)}), bf16[12,576,128]{2,1,0:T(8,128)(2,1)}, u32[]{:S(2)}, u32[]{:S(2)}) async-start(bf16[12,576,128]{2,1,0:T(8,128)(2,1)} %select_select_fusion), calls=%async_computation | async-start | bytes 3538944 | tf_op jit(solution)/shard_map/all_to_all | solution.py:150
  21.9 0.2 reshape.402
  22.1 0.6 constant_dynamic-slice_fusion.3
  22.7 0.6 fusion.60
  23.3 0.2 convert_reduce_fusion
  23.5 0.2 fusion.68
  23.8 39.4 %all-to-all-done = bf16[12,576,128]{2,1,0:T(8,128)(2,1)} async-done(((bf16[12,576,128]{2,1,0:T(8,128)(2,1)}), bf16[12,576,128]{2,1,0:T(8,128)(2,1)}, u32[]{:S(2)}, u32[]{:S(2)}) %all-to-all-start) | async-done | bytes 1769504 | tf_op jit(solution)/shard_map/all_to_all | solution.py:150
  63.2 3.5 %gather_fusion.1 = bf16[12,576,128]{2,1,0:T(8,128)(2,1)} fusion(bf16[12,576,128]{2,1,0:T(8,128)(2,1)} %all-to-all-done, s32[1024]{0:T(1024)S(1)} %pad_clamp_fusion), kind=kCustom, calls=%fused_computation.1.clone | custom fusion | bytes 3538992 | tf_op jit(solution)/shard_map/jit(_take)/gather | solution.py:151
  66.7 1.7 broadcast_select_fusion
  68.4 0.8 fusion.67
  69.3 0.6 fusion.30
  69.8 2.3 %fusion.13 = f32[12,2,64,512]{3,2,1,0:T(8,128)} fusion(bf16[12,576,128]{2,1,0:T(8,128)(2,1)S(1)} %broadcast_select_fusion, f32[12,2,64,128]{3,2,1,0:T(8,128)S(1)} %get-tuple-element.233, f32[12,2,64]{2,1,0:T(2,128)S(1)} %get-tuple-element.232, s32[12]{0:T(128)S(1)} %fusion.60), kind=kOutput, calls=%fused_computation.29 | convolution fusion | flops 202113024 | bytes 5517824 | tf_op jit(solution)/shard_map/psht,pct->pshc/dot_general | solution.py:49
  72.4 5.1 %all_gather.20 = bf16[4,1,2,64]{3,2,1,0:T(2,128)(2,1)S(1)} all-gather(bf16[1,1,2,64]{3,2,1,0:T(2,128)(2,1)S(1)} %fusion.50), channel_id=1, replica_groups=mesh['groups'=2,'dp'=4,'rep'=4] {'rep'}, dimensions={0}, use_global_device_ids=true | all-gather | bytes 1280 | tf_op jit(solution)/shard_map/all_gather | solution.py:21
  77.4 0.1 copy.29
  77.5 7.4 %fusion.7 = f32[2,64,1,512]{3,2,1,0:T(1,128)S(1)} fusion(f32[12,2,64,1]{0,3,2,1:T(1,128)S(1)} %copy.29, f32[12,2,64,512]{3,2,1,0:T(8,128)} %fusion.13), kind=kOutput, calls=%fused_computation.16 | convolution fusion | flops 9437184 | bytes 3414016 | tf_op jit(solution)/shard_map/jpsh,pshc->jshc/dot_general | solution.py:63
  84.9 0.2 fusion.25
  85.2 7.3 %all-gather = bf16[8,64,512]{2,1,0:T(8,128)(2,1)S(1)} all-gather(bf16[2,64,512]{2,1,0:T(8,128)(2,1)S(1)} %fusion.25), channel_id=2, replica_groups=mesh['groups'=2,'dp'=4,'rep'=4] {'rep'}, dimensions={0}, use_global_device_ids=true | all-gather | bytes 655360 | tf_op jit(solution)/shard_map/all_gather | solution.py:21
  92.5 5.1 %all_gather.19 = bf16[4,1,2,64]{3,2,1,0:T(2,128)(2,1)S(1)} all-gather(bf16[1,1,2,64]{3,2,1,0:T(2,128)(2,1)S(1)} %fusion.54), channel_id=1, replica_groups=mesh['groups'=2,'dp'=4,'rep'=4] {'rep'}, dimensions={0}, use_global_device_ids=true | all-gather | bytes 1280 | tf_op jit(solution)/shard_map/all_gather | solution.py:21
  97.5 0.6 while.19
  97.6 0.1 fusion.84
  97.8 0.1 fusion.84
  98.0 0.1 fusion.84
  98.1 0.1 copy.23
  98.2 1.0 fusion.38
  99.2 3.3 %all-to-all-start.1 = ((bf16[2,64,512]{2,0,1:T(2,128)(2,1)}), bf16[2,64,512]{2,0,1:T(2,128)(2,1)S(1)}, u32[]{:S(2)}, u32[]{:S(2)}) async-start(bf16[2,64,512]{2,0,1:T(2,128)(2,1)} %fusion.38), calls=%async_computation.1 | async-start | bytes 262144 | tf_op jit(solution)/shard_map/all_to_all | solution.py:160
  102.6 0.6 dynamic-slice
  103.8 5.2 %all-to-all-done.1 = bf16[2,64,512]{2,0,1:T(2,128)(2,1)S(1)} async-done(((bf16[2,64,512]{2,0,1:T(2,128)(2,1)}), bf16[2,64,512]{2,0,1:T(2,128)(2,1)S(1)}, u32[]{:S(2)}, u32[]{:S(2)}) %all-to-all-start.1) | async-done | bytes 131104 | tf_op jit(solution)/shard_map/all_to_all | solution.py:160
  109.2 4.4 %convolution_convert_fusion.3 = bf16[8,1792]{1,0:T(8,128)(2,1)S(1)} fusion(bf16[2048,1792]{1,0:T(8,128)(2,1)} %param.24, bf16[8,16,512]{2,0,1:T(8,128)(2,1)S(1)} %all_to_all.20, bf16[16,512,128]{2,1,0:T(8,128)(2,1)S(1)} %copy-done), kind=kOutput, calls=%fused_computation.21 | convolution fusion | flops 75528192 | bytes 9596928 | tf_op jit(solution)/shard_map/dot_general | solution.py:165
  113.6 17.5 %all-reduce = bf16[8,1792]{1,0:T(8,128)(2,1)S(1)} all-reduce(bf16[8,1792]{1,0:T(8,128)(2,1)S(1)} %convolution_convert_fusion.3), channel_id=3, replica_groups=mesh['groups'=2,'dp'=4,'rep'=4] {'dp'}, use_global_device_ids=true, to_apply=%region_12.14.clone | all-reduce | flops 14336 | bytes 57344
  131.1 0.1 multiply_reduce_fusion
  131.2 5.8 %psum.14 = f32[2]{0:T(128)S(1)} all-reduce(f32[2]{0:T(128)S(1)} %multiply_reduce_fusion), channel_id=1, replica_groups=mesh['groups'=2,'dp'=4,'rep'=4] {'rep'}, use_global_device_ids=true, to_apply=%region_14.16 | all-reduce | flops 2 | bytes 16 | tf_op jit(solution)/shard_map/psum | solution.py:171
  137.1 13.2 %all-gather.1 = bf16[4,2,1792]{2,1,0:T(2,128)(2,1)S(1)} all-gather(bf16[1,2,1792]{2,1,0:T(2,128)(2,1)S(1)} %fusion.43), channel_id=1, replica_groups=mesh['groups'=2,'dp'=4,'rep'=4] {'dp'}, dimensions={0}, use_global_device_ids=true | all-gather | bytes 35840 | tf_op jit(solution)/shard_map/all_gather | solution.py:175
  150.3 5.7 %convolution_convert_fusion = bf16[8,3072]{1,0:T(8,128)(2,1)S(1)} fusion(bf16[8,1792]{1,0:T(8,128)(2,1)S(1)} %reshape.433, bf16[1792,3072]{1,0:T(8,128)(2,1)} %param.28), kind=kOutput, calls=%fused_computation.18 | convolution fusion | flops 88104960 | bytes 11087872 | tf_op jit(solution)/shard_map/dot_general | solution.py:177
  156.0 5.7 %convolution_convert_fusion.1 = bf16[8,3072]{1,0:T(8,128)(2,1)S(1)} fusion(bf16[8,1792]{1,0:T(8,128)(2,1)S(1)} %reshape.433, bf16[1792,3072]{1,0:T(8,128)(2,1)} %param.27), kind=kOutput, calls=%fused_computation.19 | convolution fusion | flops 88104960 | bytes 11087872 | tf_op jit(solution)/shard_map/dot_general | solution.py:176
  161.7 0.6 pad_maximum_fusion
  162.3 30.3 %all-reduce.4.cloned.1.call-done = bf16[8,6144]{1,0:T(8,128)(2,1)} async-done(((bf16[8,6144]{1,0:T(8,128)(2,1)}), bf16[8,6144]{1,0:T(8,128)(2,1)}) %all-reduce.4.cloned.1.call-update) | async-done | bytes 98320 | tf_op jit(solution)/shard_map/psum | solution.py:179
  192.6 0.9 convert_element_type.203
  193.5 5.7 %convolution_convert_fusion.2 = bf16[8,1792]{1,0:T(8,128)(2,1)S(1)} fusion(bf16[3072,1792]{1,0:T(8,128)(2,1)} %param.29, f32[8,6144]{1,0:T(8,128)S(1)} %convert_element_type.203), kind=kOutput, calls=%fused_computation.20 | convolution fusion | flops 88242176 | bytes 11235328 | tf_op jit(solution)/shard_map/dot_general | solution.py:186
  199.2 19.0 %all-reduce.1 = bf16[8,1792]{1,0:T(8,128)(2,1)S(1)} all-reduce(bf16[8,1792]{1,0:T(8,128)(2,1)S(1)} %convolution_convert_fusion.2), channel_id=4, replica_groups=mesh['groups'=2,'dp'=4,'rep'=4] {'dp'}, use_global_device_ids=true, to_apply=%region_16.18.clone | all-reduce | flops 14336 | bytes 57344
  218.2 0.6 add_convert_fusion
  (50 shorter events, 1.0 us)
Async XLA Ops:
  6.5 102.6 %copy-start = (bf16[16,512,128]{2,1,0:T(8,128)(2,1)S(1)}, bf16[16,512,128]{2,1,0:T(8,128)(2,1)}, u32[]{:S(2)}) copy-start(bf16[16,512,128]{2,1,0:T(8,128)(2,1)} %param.23) | copy-start | bytes 6291460
  15.4 6.5 %copy-start.1 = (bf16[2,36864]{1,0:T(2,128)(2,1)S(1)}, bf16[2,36864]{1,0:T(2,128)(2,1)}, u32[]{:S(2)}) copy-start(bf16[2,36864]{1,0:T(2,128)(2,1)} %param.21) | copy-start | bytes 442372
  15.4 6.7 %copy-start.6 = (s32[4,1]{0,1:T(1,128)S(1)}, s32[4,1]{0,1:T(1,128)}, u32[]{:S(2)}) copy-start(s32[4,1]{0,1:T(1,128)} %param.20) | copy-start | bytes 52
  15.4 7.3 %copy-start.5 = (s32[4,12]{1,0:T(4,128)S(1)}, s32[4,12]{1,0:T(4,128)}, u32[]{:S(2)}) copy-start(s32[4,12]{1,0:T(4,128)} %param.18) | copy-start | bytes 580
  15.4 8.1 %copy-start.3 = (bf16[2,576]{1,0:T(2,128)(2,1)S(1)}, bf16[2,576]{1,0:T(2,128)(2,1)}, u32[]{:S(2)}) copy-start(bf16[2,576]{1,0:T(2,128)(2,1)} %param.22) | copy-start | bytes 6916
  15.4 47.8 %all-to-all-start = ((bf16[12,576,128]{2,1,0:T(8,128)(2,1)}), bf16[12,576,128]{2,1,0:T(8,128)(2,1)}, u32[]{:S(2)}, u32[]{:S(2)}) async-start(bf16[12,576,128]{2,1,0:T(8,128)(2,1)} %select_select_fusion), calls=%async_computation | async-start | bytes 3538944 | tf_op jit(solution)/shard_map/all_to_all | solution.py:150
  97.5 5.0 %copy-start.7 = (u32[32]{0:T(128)S(1)}, u32[32]{0:T(128)}, u32[]{:S(2)}) copy-start(u32[32]{0:T(128)} %constant.150) | copy-start | bytes 388
  99.2 9.8 %all-to-all-start.1 = ((bf16[2,64,512]{2,0,1:T(2,128)(2,1)}), bf16[2,64,512]{2,0,1:T(2,128)(2,1)S(1)}, u32[]{:S(2)}, u32[]{:S(2)}) async-start(bf16[2,64,512]{2,0,1:T(2,128)(2,1)} %fusion.38), calls=%async_computation.1 | async-start | bytes 262144 | tf_op jit(solution)/shard_map/all_to_all | solution.py:160
  102.5 90.1 %all-reduce.4.cloned.1.call-start = ((), (), s32[]{:S(2)}) async-start(), calls=%async_computation.2 | async-start | bytes 196608 | tf_op jit(solution)/shard_map/psum | solution.py:179
  109.2 21.9 %copy-start.2 = (bf16[2,1792]{1,0:T(2,128)(2,1)S(1)}, bf16[2,1792]{1,0:T(2,128)(2,1)}, u32[]{:S(2)}) copy-start(bf16[2,1792]{1,0:T(2,128)(2,1)} %param.25) | copy-start | bytes 21508
  109.2 27.9 %copy-start.4 = (f32[1792]{0:T(1024)S(1)}, f32[1792]{0:T(1024)}, u32[]{:S(2)}) copy-start(f32[1792]{0:T(1024)} %param.26) | copy-start | bytes 21508
Sparse Core Ops, SparseCore 0:
  162.4 30.1 all-reduce.3
where the time goes:
time: 226 us
  waiting for transfers between devices  74.9 us (33%)
  blocking collectives  72.8 us (32%)
  matrix products  32.4 us (14%)
  between operations  14.3 us (6%)
  other arithmetic  12.1 us (5%)
  starting transfers between devices  9.85 us (4%)
  local copies, waits for them, and re-layouts  9.15 us (4%)
    all_to_all x1, waiting for transfers between devices, on_device(): lax.all_to_all(outgoing, 'dp', split_axis=0, concat_axis=0, tiled=True)  39.4 us
    unnamed x2, blocking collectives  36.4 us
    psum x1, waiting for transfers between devices, on_device(): lax.psum(partial_rows.astype(jnp.bfloat16), 'rep').astype(jnp.float32)  30.3 us
    all_gather x3, blocking collectives, merged_2(): lax.all_gather(a.astype(kind), axis)  17.4 us
    all_gather x1, blocking collectives, on_device(): piece = lax.all_gather(normed, 'dp', axis=0, tiled=True)  13.2 us
    dot_general x1, matrix products, join_pages(): jnp.einsum('jpsh,pshc->jshc', factor, partial_value, precision=lax.Precis...  7.4 us
    all_to_all x1, starting transfers between devices, on_device(): lax.all_to_all(outgoing, 'dp', split_axis=0, concat_axis=0, tiled=True)  6.49 us
    psum x1, blocking collectives, on_device(): squares = lax.psum(jnp.sum(mixed_rows * mixed_rows, axis=1), 'rep')  5.84 us
  transfers between devices with their start and end apart: 3, of which 3 were waited for; matrix products, arithmetic and copies ran while one was open for 1% of the time, Pallas kernels for 0%

commit v1 on v0

--- a/solution.py
+++ b/solution.py
@@ -1,8 +1,11 @@
+import functools
 import math
 
 import jax
 import jax.numpy as jnp
 from jax import lax
+from jax.experimental import pallas as pl
+from jax.experimental.pallas import tpu as pltpu
 from jax.sharding import PartitionSpec as P
 
 D = 7168
@@ -94,6 +97,257 @@
         preferred_element_type=jnp.float32,
     )
     return (partial_value, row_peak, row_total)
+
+
+MESH = pl.DeviceIdType.MESH
+
+
+def tile_of(width):
+    for tile in (512, 256, 128):
+        if width % tile == 0:
+            return tile
+    return width
+
+
+def feed_forward_kernel(
+    dp,
+    rep,
+    headed_ref,
+    residual_ref,
+    gain_ref,
+    up_value_hbm,
+    out_proj_hbm,
+    w_gate_hbm,
+    w_up_hbm,
+    w_down_hbm,
+    out_ref,
+    up_value,
+    out_proj,
+    w_gate,
+    w_up,
+    w_down,
+    values,
+    res_buf,
+    op_buf,
+    mixed,
+    scaled,
+    sq_buf,
+    gu_buf,
+    hidden,
+    down_send,
+    down_recv,
+    weight_sem,
+    res_send,
+    res_recv,
+    op_send,
+    op_recv,
+    sq_send,
+    sq_recv,
+    gu_send,
+    gu_recv,
+    dn_send,
+    dn_recv,
+):
+    my_rank = lax.axis_index("dp")
+    my_column = lax.axis_index("rep")
+    weights = []
+    for i, (source, target) in enumerate(
+        (
+            (up_value_hbm, up_value),
+            (out_proj_hbm, out_proj),
+            (w_gate_hbm, w_gate),
+            (w_up_hbm, w_up),
+            (w_down_hbm, w_down),
+        )
+    ):
+        copy = pltpu.make_async_copy(source, target, weight_sem.at[i])
+        copy.start()
+        weights.append(copy)
+
+    barrier = pltpu.get_barrier_semaphore()
+    ranks = [lax.rem(my_rank + k, dp) for k in range(1, dp)]
+    columns = [lax.rem(my_column + k, rep) for k in range(1, rep)]
+    for peer in ranks:
+        pl.semaphore_signal(barrier, inc=1, device_id={"dp": peer}, device_id_type=MESH)
+    for peer in columns:
+        pl.semaphore_signal(barrier, inc=1, device_id={"rep": peer}, device_id_type=MESH)
+    pl.semaphore_wait(barrier, dp - 1 + rep - 1)
+
+    def to(axis, peer, source, target, send, recv):
+        return pltpu.make_async_remote_copy(
+            src_ref=source,
+            dst_ref=target,
+            send_sem=send,
+            recv_sem=recv,
+            device_id={axis: peer},
+            device_id_type=MESH,
+        )
+
+    def spread(axis, source, target, send, recv):
+        peers = ranks if axis == "dp" else columns
+        copies = [
+            to(axis, peer, source, target, send.at[k], recv.at[k]) for k, peer in enumerate(peers)
+        ]
+        for copy in copies:
+            copy.start()
+        return copies
+
+    res_copies = spread("dp", residual_ref, res_buf.at[my_rank], res_send, res_recv)
+    res_buf[my_rank] = residual_ref[...]
+
+    heads, rows, _ = headed_ref.shape
+    rows_here, width = residual_ref.shape
+    vdim = up_value.shape[2]
+    weights[0].wait()
+    for h in range(heads):
+        values[:, h * vdim : (h + 1) * vdim] = jnp.dot(
+            headed_ref[h], up_value[h], preferred_element_type=jnp.float32
+        ).astype(jnp.bfloat16)
+
+    weights[1].wait()
+    tile = tile_of(width)
+
+    def project(i, carry):
+        at = pl.ds(pl.multiple_of(i * tile, tile), tile)
+        op_buf[my_rank, :, at] = jnp.dot(
+            values[...], out_proj[:, at], preferred_element_type=jnp.float32
+        ).astype(jnp.bfloat16)
+        return carry
+
+    lax.fori_loop(0, width // tile, project, 0)
+    op_copies = spread("dp", op_buf.at[my_rank], op_buf.at[my_rank], op_send, op_recv)
+    for copy in res_copies:
+        copy.wait()
+    for copy in op_copies:
+        copy.wait()
+    attn_out = op_buf[0].astype(jnp.float32)
+    for source in range(1, dp):
+        attn_out += op_buf[source].astype(jnp.float32)
+    squares = []
+    for source in range(dp):
+        part = attn_out[source * rows_here : (source + 1) * rows_here]
+        mixed[source] = res_buf[source].astype(jnp.float32) + part
+    whole = jnp.concatenate([mixed[source] for source in range(dp)], axis=0)
+    squares = jnp.sum(whole * whole, axis=1, keepdims=True)
+    sq_buf[my_column] = jnp.broadcast_to(squares, (rows, 128))
+    sq_copies = spread("rep", sq_buf.at[my_column], sq_buf.at[my_column], sq_send, sq_recv)
+    scaled[...] = (whole * gain_ref[...]).astype(jnp.bfloat16)
+
+    chunks, chunk = gu_buf.shape[1], gu_buf.shape[4]
+    step = tile_of(chunk)
+    weights[2].wait()
+    weights[3].wait()
+    gu_copies = []
+    for c in range(chunks):
+
+        def gate_up(i, carry):
+            at = pl.ds(pl.multiple_of(i * step, step), step)
+            source = pl.ds(pl.multiple_of(c * chunk + i * step, step), step)
+            gu_buf[my_column, c, 0, :, at] = jnp.dot(
+                scaled[...], w_gate[:, source], preferred_element_type=jnp.float32
+            ).astype(jnp.bfloat16)
+            gu_buf[my_column, c, 1, :, at] = jnp.dot(
+                scaled[...], w_up[:, source], preferred_element_type=jnp.float32
+            ).astype(jnp.bfloat16)
+            return carry
+
+        lax.fori_loop(0, chunk // step, gate_up, 0)
+        block = gu_buf.at[my_column, c]
+        gu_copies.append(spread("rep", block, block, gu_send.at[c], gu_recv.at[c]))
+
+    for copy in sq_copies:
+        copy.wait()
+    total = sq_buf[0]
+    for source in range(1, rep):
+        total += sq_buf[source]
+    scale = lax.rsqrt(total[:, :1] / D + epsilon)
+    for c in range(chunks):
+        for copy in gu_copies[c]:
+            copy.wait()
+        gate = gu_buf[0, c, 0].astype(jnp.float32)
+        up = gu_buf[0, c, 1].astype(jnp.float32)
+        for source in range(1, rep):
+            gate += gu_buf[source, c, 0].astype(jnp.float32)
+            up += gu_buf[source, c, 1].astype(jnp.float32)
+        gate = gate * scale
+        up = up * scale
+        hidden[:, c * chunk : (c + 1) * chunk] = (gate / (1.0 + jnp.exp(-gate)) * up).astype(
+            jnp.bfloat16
+        )
+
+    weights[4].wait()
+
+    def project_down(i, carry):
+        at = pl.ds(pl.multiple_of(i * tile, tile), tile)
+        part = jnp.dot(hidden[...], w_down[:, at], preferred_element_type=jnp.float32).astype(
+            jnp.bfloat16
+        )
+        for p in range(dp):
+            down_send[p, :, at] = part[p * rows_here : (p + 1) * rows_here]
+        return carry
+
+    lax.fori_loop(0, width // tile, project_down, 0)
+    dn_copies = [
+        to("dp", peer, down_send.at[peer], down_recv.at[my_rank], dn_send.at[k], dn_recv.at[k])
+        for k, peer in enumerate(ranks)
+    ]
+    for copy in dn_copies:
+        copy.start()
+    result = mixed[my_rank] + down_send[my_rank].astype(jnp.float32)
+    for copy in dn_copies:
+        copy.wait()
+    for peer in ranks:
+        result += down_recv[peer].astype(jnp.float32)
+    out_ref[...] = result.astype(jnp.bfloat16)
+
+
+def feed_forward(headed, residual, norm_gain, up_value, out_proj, w_gate, w_up, w_down):
+    dp, rep = lax.axis_size("dp"), lax.axis_size("rep")
+    heads, rows, _ = headed.shape
+    rows_here, width = residual.shape
+    inner, hidden_width = out_proj.shape[0], w_gate.shape[1]
+    chunks = 3 if hidden_width % (3 * 128) == 0 else 1
+    bf16, f32 = jnp.bfloat16, jnp.float32
+    dma = pltpu.SemaphoreType.DMA
+    vmem = pl.BlockSpec(memory_space=pltpu.VMEM)
+    hbm = pl.BlockSpec(memory_space=pl.ANY)
+    return pl.pallas_call(
+        functools.partial(feed_forward_kernel, dp, rep),
+        out_shape=jax.ShapeDtypeStruct((rows_here, width), bf16),
+        in_specs=[vmem, vmem, vmem] + [hbm] * 5,
+        out_specs=vmem,
+        scratch_shapes=[
+            pltpu.VMEM(up_value.shape, bf16),
+            pltpu.VMEM(out_proj.shape, bf16),
+            pltpu.VMEM(w_gate.shape, bf16),
+            pltpu.VMEM(w_up.shape, bf16),
+            pltpu.VMEM(w_down.shape, bf16),
+            pltpu.VMEM((rows, inner), bf16),
+            pltpu.VMEM((dp, rows_here, width), bf16),
+            pltpu.VMEM((dp, rows, width), bf16),
+            pltpu.VMEM((dp, rows_here, width), f32),
+            pltpu.VMEM((rows, width), bf16),
+            pltpu.VMEM((rep, rows, 128), f32),
+            pltpu.VMEM((rep, chunks, 2, rows, hidden_width // chunks), bf16),
+            pltpu.VMEM((rows, hidden_width), bf16),
+            pltpu.VMEM((dp, rows_here, width), bf16),
+            pltpu.VMEM((dp, rows_here, width), bf16),
+            dma((5,)),
+            dma((dp - 1,)),
+            dma((dp - 1,)),
+            dma((dp - 1,)),
+            dma((dp - 1,)),
+            dma((rep - 1,)),
+            dma((rep - 1,)),
+            dma((chunks, rep - 1)),
+            dma((chunks, rep - 1)),
+            dma((dp - 1,)),
+            dma((dp - 1,)),
+        ],
+        compiler_params=pltpu.CompilerParams(
+            collective_id=0, has_side_effects=True, vmem_limit_bytes=60 * 1024 * 1024
+        ),
+    )(headed, residual, norm_gain.reshape(1, -1), up_value, out_proj, w_gate, w_up, w_down)
 
 
 def on_device(
@@ -158,37 +412,16 @@
         (merged[0] / merged[2][..., None]).astype(jnp.bfloat16).reshape(rows_here, head_count, CKV)
     )
     headed = lax.all_to_all(attention, "dp", split_axis=1, concat_axis=0, tiled=True)
-    values = jnp.einsum("rhc,hcv->rhv", headed, up_value, preferred_element_type=jnp.float32)
-    values = values.astype(jnp.bfloat16).reshape(headed.shape[0], -1)
-    picked = values
-    attn_out = lax.psum_scatter(
-        jnp.dot(picked, out_proj, preferred_element_type=jnp.float32).astype(jnp.bfloat16),
-        "dp",
-        scatter_dimension=0,
-        tiled=True,
-    ).astype(jnp.float32)
-    mixed_rows = residual.astype(jnp.float32) + attn_out
-    squares = lax.psum(jnp.sum(mixed_rows * mixed_rows, axis=1), "rep")
-    normed = (mixed_rows * lax.rsqrt(squares / D + epsilon)[:, None] * norm_gain).astype(
-        jnp.bfloat16
-    )
-    piece = lax.all_gather(normed, "dp", axis=0, tiled=True)
-    gate_part = jnp.dot(piece, w_gate, preferred_element_type=jnp.float32)
-    up_part = jnp.dot(piece, w_up, preferred_element_type=jnp.float32)
-    partial_rows = jnp.concatenate([gate_part, up_part], axis=1)
-    gate_up = lax.psum(partial_rows.astype(jnp.bfloat16), "rep").astype(jnp.float32)
-    hidden_width = w_gate.shape[1]
-    hidden = (jax.nn.silu(gate_up[:, :hidden_width]) * gate_up[:, hidden_width:]).astype(
-        jnp.bfloat16
-    )
-    picked = hidden
-    mlp_out = lax.psum_scatter(
-        jnp.dot(picked, w_down, preferred_element_type=jnp.float32).astype(jnp.bfloat16),
-        "dp",
-        scatter_dimension=0,
-        tiled=True,
-    ).astype(jnp.float32)
-    return (mixed_rows + mlp_out).astype(jnp.bfloat16)
+    return feed_forward(
+        headed.transpose(1, 0, 2),
+        residual,
+        norm_gain,
+        up_value,
+        out_proj,
+        w_gate,
+        w_up,
+        w_down,
+    )
 
 
 def solution(mesh):

time: 226 us -> 125 us (0.55)
  blocking collectives: 72.8 us -> 17.4 us
  waiting for transfers between devices: 74.9 us -> 40.8 us
  Pallas kernels: 0 us -> 24.9 us
  matrix products: 32.4 us -> 11.9 us
  between operations: 14.3 us -> 0.17 us
    unnamed x2 -> x0, blocking collectives: 36.4 us -> none
    psum x1 -> x0, waiting for transfers between devices: 30.3 us -> none  [on_device(): lax.psum(partial_rows.astype(jnp.bfloat16), 'rep').astype(jnp.float32)]
    pallas_call x0 -> x1, Pallas kernels: none -> 24.9 us  [feed_forward(): pl.pallas_call(functools.partial(feed_forward_kernel, dp, rep), out_shape...]
    dot_general x4 -> x0, matrix products: 21.4 us -> none  [the longest x1 5.67 us: on_device(): gate_part = jnp.dot(piece, w_gate, preferred_element_type=jnp.float32)]
    all_gather x1 -> x0, blocking collectives: 13.2 us -> none  [on_device(): piece = lax.all_gather(normed, 'dp', axis=0, tiled=True)]
    psum x1 -> x0, blocking collectives: 5.84 us -> none  [on_device(): squares = lax.psum(jnp.sum(mixed_rows * mixed_rows, axis=1), 'rep')]
    all_to_all x1, waiting for transfers between devices: 39.4 us -> 35.1 us  [on_device(): lax.all_to_all(outgoing, 'dp', split_axis=0, concat_axis=0, tiled=True)]
    gather x1, local copies, waits for them, and re-layouts: 3.51 us -> 0.89 us  [on_device(): outgoing = jnp.take(stored, sent_page, axis=0)]
  transfers between devices with their start and end apart: 3 -> 2, of which waited for: 3 -> 2; matrix products, arithmetic and copies ran while one was open for 1% -> 5% of each run, Pallas kernels for 0% -> 0%
where the time goes in v1:
time: 125 us; the launch traced here: 124 us
  waiting for transfers between devices  40.8 us (33%)
  Pallas kernels  24.9 us (20%)
  blocking collectives  17.4 us (14%)
  matrix products  11.9 us (10%)
  other arithmetic  10.6 us (8%)
  starting transfers between devices  9.98 us (8%)
  local copies, waits for them, and re-layouts  8.59 us (7%)
    all_to_all x1, waiting for transfers between devices, on_device(): lax.all_to_all(outgoing, 'dp', split_axis=0, concat_axis=0, tiled=True)  35.1 us
    pallas_call x1, Pallas kernels, feed_forward(): pl.pallas_call(functools.partial(feed_forward_kernel, dp, rep), out_shape...  24.9 us
    all_gather x3, blocking collectives, merged_2(): lax.all_gather(a.astype(kind), axis)  17.4 us
    dot_general x1, matrix products, join_pages(): jnp.einsum('jpsh,pshc->jshc', factor, partial_value, precision=lax.Precis...  7.4 us
    all_to_all x1, starting transfers between devices, on_device(): lax.all_to_all(outgoing, 'dp', split_axis=0, concat_axis=0, tiled=True)  6.48 us
    all_to_all x1, waiting for transfers between devices, on_device(): lax.all_to_all(attention, 'dp', split_axis=1, concat_axis=0, tiled=True)  5.67 us
    all_to_all x1, starting transfers between devices, on_device(): lax.all_to_all(attention, 'dp', split_axis=1, concat_axis=0, tiled=True)  3.5 us
  transfers between devices with their start and end apart: 2, of which 2 were waited for; matrix products, arithmetic and copies ran while one was open for 5% of the time, Pallas kernels for 0%

profile of v1, /device:TPU:0, one launch (start us, length us, event | category | flops | bytes accessed | tf_op | source)
XLA Modules:
  0.0 124.4 jit_solution(7585520024450182681)
XLA Ops:
  0.0 0.8 fusion.60
  0.8 0.2 reduce_window_sum.11
  1.0 0.1 fusion.40
  1.2 0.8 select_reduce_fusion.1
  2.0 0.1 copy.21
  2.1 0.1 reshape.394
  2.2 0.5 compare_and_fusion.2
  2.7 0.1 copy.20
  2.8 0.1 broadcast_in_dim.120
  2.9 0.9 gather_fusion
  3.8 1.5 %select_select_fusion = bf16[12,576,128]{2,1,0:T(8,128)(2,1)} fusion(bf16[12,576,128]{2,1,0:T(8,128)(2,1)S(1)} %gather_fusion, pred[12]{0:T(512)(128)(4,1)S(1)} %get-tuple-element.237, pred[12]{0:T(512)(128)(4,1)S(1)} %broadcast_in_dim.120), kind=kLoop, calls=%fused_computation.22 | loop fusion | flops 1769472 | bytes 3538968 | tf_op jit(solution)/shard_map/jit(_where)/select_n | solution.py:403
  5.3 6.5 %all-to-all-start = ((bf16[12,576,128]{2,1,0:T(8,128)(2,1)}), bf16[12,576,128]{2,1,0:T(8,128)(2,1)S(1)}, u32[]{:S(2)}, u32[]{:S(2)}) async-start(bf16[12,576,128]{2,1,0:T(8,128)(2,1)} %select_select_fusion), calls=%async_computation | async-start | bytes 3538944 | tf_op jit(solution)/shard_map/all_to_all | solution.py:404
  11.8 1.8 %reshape.400 = bf16[2,64,576]{2,1,0:T(8,128)(2,1)} reshape(bf16[2,36864]{1,0:T(2,128)(2,1)} %param.21) | data formatting | bytes 294912 | tf_op jit(solution)/shard_map/jit(_take)/gather | solution.py:406
  13.6 0.0 copy-done.9
  13.6 0.6 constant_dynamic-slice_fusion.2
  14.2 1.2 fusion.55
  15.3 0.2 convert_reduce_fusion
  15.5 0.6 compare_and_fusion.1
  16.1 1.1 fusion.62
  17.3 0.6 fusion.58
  17.9 35.1 %all-to-all-done = bf16[12,576,128]{2,1,0:T(8,128)(2,1)S(1)} async-done(((bf16[12,576,128]{2,1,0:T(8,128)(2,1)}), bf16[12,576,128]{2,1,0:T(8,128)(2,1)S(1)}, u32[]{:S(2)}, u32[]{:S(2)}) %all-to-all-start) | async-done | bytes 1769504 | tf_op jit(solution)/shard_map/all_to_all | solution.py:404
  53.0 2.0 %gather_fusion.1 = bf16[12,576,128]{2,1,0:T(8,128)(2,1)} fusion(bf16[12,576,128]{2,1,0:T(8,128)(2,1)S(1)} %all-to-all-done, s32[1024]{0:T(1024)S(1)} %pad_clamp_fusion), kind=kCustom, calls=%fused_computation.1.clone | custom fusion | bytes 3538992 | tf_op jit(solution)/shard_map/jit(_take)/gather | solution.py:405
  55.0 1.7 %broadcast_select_fusion = bf16[12,576,128]{2,1,0:T(8,128)(2,1)S(1)} fusion(bf16[12,576,128]{2,1,0:T(8,128)(2,1)} %gather_fusion.1, pred[12]{0:T(512)(128)(4,1)} %get-tuple-element.222), kind=kLoop, calls=%fused_computation.23 | loop fusion | flops 884736 | bytes 3538956 | tf_op jit(solution)/shard_map/jit(_take)/select_n | solution.py:405
  56.8 0.8 fusion.61
  57.6 0.6 fusion.29
  58.2 0.0 copy-start.5
  58.2 2.3 %fusion.13 = f32[12,2,64,512]{3,2,1,0:T(8,128)} fusion(bf16[12,576,128]{2,1,0:T(8,128)(2,1)S(1)} %broadcast_select_fusion, f32[12,2,64,128]{3,2,1,0:T(8,128)S(1)} %get-tuple-element.233, f32[12,2,64]{2,1,0:T(2,128)S(1)} %get-tuple-element.232, s32[12]{0:T(128)S(1)} %copy-done.7), kind=kOutput, calls=%fused_computation.25 | convolution fusion | flops 202113024 | bytes 5517824 | tf_op jit(solution)/shard_map/psht,pct->pshc/dot_general | solution.py:52
  60.5 0.1 select_reduce_fusion
  60.7 0.1 multiply_reduce_fusion
  60.8 5.1 %all_gather.17 = bf16[4,1,2,64]{3,2,1,0:T(2,128)(2,1)S(1)} all-gather(bf16[1,1,2,64]{3,2,1,0:T(2,128)(2,1)S(1)} %fusion.45), channel_id=1, replica_groups=mesh['groups'=2,'dp'=4,'rep'=4] {'rep'}, dimensions={0}, use_global_device_ids=true | all-gather | bytes 1280 | tf_op jit(solution)/shard_map/all_gather | solution.py:24
  65.8 0.1 copy.29
  65.9 7.4 %fusion.7 = f32[2,64,1,512]{3,2,1,0:T(1,128)S(1)} fusion(f32[12,2,64,1]{0,3,2,1:T(1,128)S(1)} %copy.29, f32[12,2,64,512]{3,2,1,0:T(8,128)} %fusion.13), kind=kOutput, calls=%fused_computation.16 | convolution fusion | flops 9437184 | bytes 3414016 | tf_op jit(solution)/shard_map/jpsh,pshc->jshc/dot_general | solution.py:66
  73.3 0.2 fusion.25
  73.6 7.3 %all-gather = bf16[8,64,512]{2,1,0:T(8,128)(2,1)S(1)} all-gather(bf16[2,64,512]{2,1,0:T(8,128)(2,1)S(1)} %fusion.25), channel_id=2, replica_groups=mesh['groups'=2,'dp'=4,'rep'=4] {'rep'}, dimensions={0}, use_global_device_ids=true | all-gather | bytes 655360 | tf_op jit(solution)/shard_map/all_gather | solution.py:24
  80.9 5.1 %all_gather.16 = bf16[4,1,2,64]{3,2,1,0:T(2,128)(2,1)S(1)} all-gather(bf16[1,1,2,64]{3,2,1,0:T(2,128)(2,1)S(1)} %fusion.49), channel_id=1, replica_groups=mesh['groups'=2,'dp'=4,'rep'=4] {'rep'}, dimensions={0}, use_global_device_ids=true | all-gather | bytes 1280 | tf_op jit(solution)/shard_map/all_gather | solution.py:24
  86.0 0.6 while.19
  86.0 0.1 fusion.70
  86.2 0.1 fusion.70
  86.4 0.1 fusion.70
  86.6 0.1 copy.23
  86.6 1.0 fusion.37
  87.6 3.5 %all-to-all-start.1 = ((bf16[2,64,512]{2,0,1:T(2,128)(2,1)}), bf16[2,64,512]{2,0,1:T(2,128)(2,1)S(1)}, u32[]{:S(2)}, u32[]{:S(2)}) async-start(bf16[2,64,512]{2,0,1:T(2,128)(2,1)} %fusion.37), calls=%async_computation.1 | async-start | bytes 262144 | tf_op jit(solution)/shard_map/all_to_all | solution.py:414
  91.1 0.6 reshape.399.gain_ref
  91.7 5.7 %all-to-all-done.1 = bf16[2,64,512]{2,0,1:T(2,128)(2,1)S(1)} async-done(((bf16[2,64,512]{2,0,1:T(2,128)(2,1)}), bf16[2,64,512]{2,0,1:T(2,128)(2,1)S(1)}, u32[]{:S(2)}, u32[]{:S(2)}) %all-to-all-start.1) | async-done | bytes 131104 | tf_op jit(solution)/shard_map/all_to_all | solution.py:414
  97.4 0.1 copy.40
  97.5 0.7 all_to_all.20
  98.2 24.9 %shard_map.127 = bf16[2,1792]{1,0:T(2,128)(2,1)} custom-call(bf16[16,8,512]{2,1,0:T(8,128)(2,1)} %bitcast.130, bf16[2,1792]{1,0:T(2,128)(2,1)} %residual_ref.1, f32[1,1792]{1,0:T(1,128)} %reshape.399.gain_ref, bf16[16,512,128]{2,1,0:T(8,128)(2,1)} %up_value_hbm.1, bf16[2048,1792]{1,0:T(8,128)(2,1)} %out_proj_hbm.1, bf16[1792,3072]{1,0:T(8,128)(2,1)} %w_gate_hbm.1, ...), custom_call_target="tpu_custom_call" | custom-call | tf_op jit(solution)/shard_map/pallas_call | solution.py:314
  123.1 1.3 %copy.54 = bf16[2,1792]{1,0:T(2,128)(2,1)} copy(bf16[2,1792]{1,0:T(2,128)(2,1)} %shard_map.127) | data formatting | bytes 14336
  (38 shorter events, 0.2 us)
Async XLA Ops:
  0.0 2.9 %copy-start = (bf16[1,12,576,128]{3,2,1,0:T(8,128)(2,1)S(1)}, bf16[1,12,576,128]{3,2,1,0:T(8,128)(2,1)}, u32[]{:S(2)}) copy-start(bf16[1,12,576,128]{3,2,1,0:T(8,128)(2,1)} %param.17) | copy-start | bytes 5308420
  5.3 8.3 %copy-start.9 = (s32[4,1]{0,1:T(1,128)S(1)}, s32[4,1]{0,1:T(1,128)}, u32[]{:S(2)}) copy-start(s32[4,1]{0,1:T(1,128)} %param.20) | copy-start | bytes 52
  5.3 8.8 %copy-start.6 = (s32[4,12]{1,0:T(4,128)S(1)}, s32[4,12]{1,0:T(4,128)}, u32[]{:S(2)}) copy-start(s32[4,12]{1,0:T(4,128)} %param.18) | copy-start | bytes 580
  5.3 10.8 %copy-start.2 = (bf16[2,576]{1,0:T(2,128)(2,1)S(1)}, bf16[2,576]{1,0:T(2,128)(2,1)}, u32[]{:S(2)}) copy-start(bf16[2,576]{1,0:T(2,128)(2,1)} %param.22) | copy-start | bytes 6916
  5.3 47.7 %all-to-all-start = ((bf16[12,576,128]{2,1,0:T(8,128)(2,1)}), bf16[12,576,128]{2,1,0:T(8,128)(2,1)S(1)}, u32[]{:S(2)}, u32[]{:S(2)}) async-start(bf16[12,576,128]{2,1,0:T(8,128)(2,1)} %select_select_fusion), calls=%async_computation | async-start | bytes 3538944 | tf_op jit(solution)/shard_map/all_to_all | solution.py:404
  55.0 1.8 %copy-start.1 = (bf16[2,64,576]{2,1,0:T(8,128)(2,1)S(1)}, bf16[2,64,576]{2,1,0:T(8,128)(2,1)}, u32[]{:S(2)}) copy-start(bf16[2,64,576]{2,1,0:T(8,128)(2,1)} %reshape.400) | copy-start | bytes 442372
  55.0 1.8 %copy-start.7 = (s32[12]{0:T(128)S(1)}, s32[12]{0:T(128)}, u32[]{:S(2)}) copy-start(s32[12]{0:T(128)} %fusion.55) | copy-start | bytes 148
  55.0 1.8 %copy-start.8 = (pred[12]{0:T(512)(128)(4,1)S(1)}, pred[12]{0:T(512)(128)(4,1)}, u32[]{:S(2)}) copy-start(pred[12]{0:T(512)(128)(4,1)} %get-tuple-element.236) | copy-start | bytes 40
  58.2 2.3 %copy-start.4 = (pred[12]{0:T(512)(128)(4,1)S(1)}, pred[12]{0:T(512)(128)(4,1)}, u32[]{:S(2)}) copy-start(pred[12]{0:T(512)(128)(4,1)} %get-tuple-element.238) | copy-start | bytes 40
  58.2 2.5 %copy-start.5 = (f32[2,64]{1,0:T(2,128)S(1)}, f32[2,64]{1,0:T(2,128)}, u32[]{:S(2)}) copy-start(f32[2,64]{1,0:T(2,128)} %fusion.58) | copy-start | bytes 1540
  86.0 5.2 %copy-start.3 = (f32[1792]{0:T(1024)S(1)}, f32[1792]{0:T(1024)}, u32[]{:S(2)}) copy-start(f32[1792]{0:T(1024)} %param.26) | copy-start | bytes 21508
  87.6 9.8 %all-to-all-start.1 = ((bf16[2,64,512]{2,0,1:T(2,128)(2,1)}), bf16[2,64,512]{2,0,1:T(2,128)(2,1)S(1)}, u32[]{:S(2)}, u32[]{:S(2)}) async-start(bf16[2,64,512]{2,0,1:T(2,128)(2,1)} %fusion.37), calls=%async_computation.1 | async-start | bytes 262144 | tf_op jit(solution)/shard_map/all_to_all | solution.py:414

commit v2 on v1

v2 whole, which is shorter than its diff:
```python
import functools
import math

import jax
import jax.numpy as jnp
from jax import lax
from jax.experimental import pallas as pl
from jax.experimental.pallas import tpu as pltpu
from jax.sharding import PartitionSpec as P

D = 7168
CKV = 512
PAGE = 128
PAGES = 48


score_scale = 1.0 / math.sqrt(192.0)
epsilon = 1e-06
mask_value = -1e30


MESH = pl.DeviceIdType.MESH


def tile_of(width):
    for tile in (512, 256, 128):
        if width % tile == 0:
            return tile
    return width


def layer_kernel(
    dp,
    rep,
    query_ref,
    fresh_ref,
    bias_ref,
    residual_ref,
    gain_ref,
    store_hbm,
    up_value_hbm,
    out_proj_hbm,
    w_gate_hbm,
    w_up_hbm,
    w_down_hbm,
    out_ref,
    pages,
    queries,
    scores,
    part,
    part_stat,
    part_recv,
    stat_recv,
    share,
    share_stat,
    share_recv,
    share_stat_recv,
    value_buf,
    up_value,
    out_proj,
    w_gate,
    w_up,
    w_down,
    values,
    res_buf,
    op_buf,
    mixed,
    scaled,
    sq_buf,
    gu_buf,
    hidden,
    down_send,
    down_recv,
    weight_sem,
    q_send,
    q_recv,
    f_send,
    f_recv,
    p_send,
    p_recv,
    s_send,
    s_recv,
    v_send,
    v_recv,
    res_send,
    res_recv,
    op_send,
    op_recv,
    sq_send,
    sq_recv,
    gu_send,
    gu_recv,
    dn_send,
    dn_recv,
):
    my_rank = lax.axis_index("dp")
    my_column = lax.axis_index("rep")
    weights = []
    for i, (source, target) in enumerate(
        (
            (store_hbm.at[0], pages),
            (up_value_hbm, up_value),
            (out_proj_hbm, out_proj),
            (w_gate_hbm, w_gate),
            (w_up_hbm, w_up),
            (w_down_hbm, w_down),
        )
    ):
        copy = pltpu.make_async_copy(source, target, weight_sem.at[i])
        copy.start()
        weights.append(copy)

    barrier = pltpu.get_barrier_semaphore()
    ranks = [lax.rem(my_rank + k, dp) for k in range(1, dp)]
    columns = [lax.rem(my_column + k, rep) for k in range(1, rep)]
    for peer in ranks:
        pl.semaphore_signal(barrier, inc=1, device_id={"dp": peer}, device_id_type=MESH)
    for peer in columns:
        pl.semaphore_signal(barrier, inc=1, device_id={"rep": peer}, device_id_type=MESH)
    pl.semaphore_wait(barrier, dp - 1 + rep - 1)

    def to(axis, peer, source, target, send, recv):
        return pltpu.make_async_remote_copy(
            src_ref=source,
            dst_ref=target,
            send_sem=send,
            recv_sem=recv,
            device_id={axis: peer},
            device_id_type=MESH,
        )

    def spread(axis, source, target, send, recv):
        peers = ranks if axis == "dp" else columns
        copies = [
            to(axis, peer, source, target, send.at[k], recv.at[k]) for k, peer in enumerate(peers)
        ]
        for copy in copies:
            copy.start()
        return copies

    res_copies = spread("dp", residual_ref, res_buf.at[my_rank], res_send, res_recv)
    res_buf[my_rank] = residual_ref[...]

    q_copies = spread("dp", query_ref.at[my_column], queries.at[my_rank, my_column], q_send, q_recv)
    queries[my_rank] = query_ref[...]
    f_copies = []
    for k, copy in enumerate(q_copies):
        copy.wait()
        block = queries.at[lax.rem(my_rank + dp - 1 - k, dp), my_column]
        f_copies.append(spread("rep", block, block, f_send.at[k], f_recv.at[k]))
    for copies in f_copies:
        for copy in copies:
            copy.wait()

    rows_here, width = residual_ref.shape
    rows = dp * rows_here
    page_count, latent_width, page = pages.shape
    query_count = rep * query_ref.shape[1]
    group = dp // rep
    share_rows = query_count // dp
    weights[0].wait()
    row_ids = lax.broadcasted_iota(jnp.int32, (query_count, 1), 0) % rows_here
    lanes = lax.broadcasted_iota(jnp.int32, (query_count, 128), 1)

    def attend(d, carry):
        query = queries[d].reshape(query_count, latent_width)
        for p in range(page_count + 1):
            keys = pages[p] if p < page_count else fresh_ref[...]
            scores[:, p * page : (p + 1) * page] = jnp.dot(
                query, keys, preferred_element_type=jnp.float32
            )
        bias = bias_ref[d]
        limit = bias[0:1]
        for r in range(1, rows_here):
            limit = jnp.where(row_ids == r, bias[r : r + 1], limit)
        visible = limit > 0.5
        score = jnp.where(visible, scores[...] * score_scale, mask_value)
        peak = jnp.max(score, axis=1, keepdims=True)
        weight = jnp.where(visible, jnp.exp(score - peak), 0.0)
        total = jnp.sum(weight, axis=1, keepdims=True)
        weight = weight.astype(jnp.bfloat16)
        value = jnp.zeros((query_count, CKV), jnp.float32)
        for p in range(page_count + 1):
            keys = pages[p, :CKV] if p < page_count else fresh_ref[:CKV]
            value += lax.dot_general(
                weight[:, p * page : (p + 1) * page],
                keys,
                (((1,), (1,)), ((), ())),
                preferred_element_type=jnp.float32,
            )
        part[d // group, d % group] = value.astype(jnp.bfloat16)
        both = jnp.where(lanes % 2 == 0, peak, total)
        part_stat[d // group, d % group] = both.T[:8]
        return carry

    lax.fori_loop(0, dp, attend, 0)

    p_copies = []
    for k, peer in enumerate(columns):
        for j, (source, target) in enumerate(((part, part_recv), (part_stat, stat_recv))):
            copy = to(
                "rep",
                peer,
                source.at[peer],
                target.at[my_column],
                p_send.at[j, k],
                p_recv.at[j, k],
            )
            copy.start()
            p_copies.append(copy)
    part_recv[my_column] = part[my_column]
    stat_recv[my_column] = part_stat[my_column]
    for copy in p_copies:
        copy.wait()
    for g in range(group):
        peaks, totals = [], []
        for c in range(rep):
            stat = stat_recv[c, g]
            peaks.append(jnp.broadcast_to(stat[0:1], (128, query_count)).T[:, :1])
            totals.append(jnp.broadcast_to(stat[1:2], (128, query_count)).T[:, :1])
        best = functools.reduce(jnp.maximum, peaks)
        value = jnp.zeros((query_count, CKV), jnp.float32)
        total = jnp.zeros((query_count, 1), jnp.float32)
        for c in range(rep):
            factor = jnp.exp(peaks[c] - best)
            value += part_recv[c, g].astype(jnp.float32) * factor
            total += totals[c] * factor
        value = value.astype(jnp.bfloat16)
        both = jnp.where(lanes % 2 == 0, best, total)
        for p in range(dp):
            share[p, g] = value[p * share_rows : (p + 1) * share_rows]
            share_stat[p, g] = both[p * share_rows : (p + 1) * share_rows]

    s_copies = []
    for k, peer in enumerate(ranks):
        for j, (source, target) in enumerate(((share, share_recv), (share_stat, share_stat_recv))):
            copy = to(
                "dp",
                peer,
                source.at[peer],
                target.at[my_rank],
                s_send.at[j, k],
                s_recv.at[j, k],
            )
            copy.start()
            s_copies.append(copy)
    share_recv[my_rank] = share[my_rank]
    share_stat_recv[my_rank] = share_stat[my_rank]
    for copy in s_copies:
        copy.wait()
    heads = up_value.shape[0]
    vdim = up_value.shape[2]
    weights[1].wait()
    for g in range(group):
        best = share_stat_recv[0, g][:, 0:1]
        for p in range(1, dp):
            best = jnp.maximum(best, share_stat_recv[p, g][:, 0:1])
        value = jnp.zeros((share_rows, CKV), jnp.float32)
        total = jnp.zeros((share_rows, 1), jnp.float32)
        for p in range(dp):
            factor = jnp.exp(share_stat_recv[p, g][:, 0:1] - best)
            value += share_recv[p, g].astype(jnp.float32) * factor
            total += share_stat_recv[p, g][:, 1:2] * factor
        latent = (value / total).astype(jnp.bfloat16)
        for h in range(heads):
            value_buf[my_column, g, :, h * vdim : (h + 1) * vdim] = jnp.dot(
                latent[h * rows_here : (h + 1) * rows_here],
                up_value[h],
                preferred_element_type=jnp.float32,
            ).astype(jnp.bfloat16)
    for copy in spread(
        "rep", value_buf.at[my_column], value_buf.at[my_column], v_send, v_recv
    ):
        copy.wait()
    values[...] = jnp.concatenate(
        [value_buf[c, g].astype(jnp.float32) for c in range(rep) for g in range(group)], axis=0
    ).astype(jnp.bfloat16)

    weights[2].wait()
    tile = tile_of(width)

    def project(i, carry):
        at = pl.ds(pl.multiple_of(i * tile, tile), tile)
        op_buf[my_rank, :, at] = jnp.dot(
            values[...], out_proj[:, at], preferred_element_type=jnp.float32
        ).astype(jnp.bfloat16)
        return carry

    lax.fori_loop(0, width // tile, project, 0)
    op_copies = spread("dp", op_buf.at[my_rank], op_buf.at[my_rank], op_send, op_recv)
    for copy in res_copies:
        copy.wait()
    for copy in op_copies:
        copy.wait()
    attn_out = op_buf[0].astype(jnp.float32)
    for source in range(1, dp):
        attn_out += op_buf[source].astype(jnp.float32)
    squares = []
    for source in range(dp):
        part = attn_out[source * rows_here : (source + 1) * rows_here]
        mixed[source] = res_buf[source].astype(jnp.float32) + part
    whole = jnp.concatenate([mixed[source] for source in range(dp)], axis=0)
    squares = jnp.sum(whole * whole, axis=1, keepdims=True)
    sq_buf[my_column] = jnp.broadcast_to(squares, (rows, 128))
    sq_copies = spread("rep", sq_buf.at[my_column], sq_buf.at[my_column], sq_send, sq_recv)
    scaled[...] = (whole * gain_ref[...]).astype(jnp.bfloat16)

    chunks, chunk = gu_buf.shape[1], gu_buf.shape[4]
    step = tile_of(chunk)
    weights[3].wait()
    weights[4].wait()
    gu_copies = []
    for c in range(chunks):

        def gate_up(i, carry):
            at = pl.ds(pl.multiple_of(i * step, step), step)
            source = pl.ds(pl.multiple_of(c * chunk + i * step, step), step)
            gu_buf[my_column, c, 0, :, at] = jnp.dot(
                scaled[...], w_gate[:, source], preferred_element_type=jnp.float32
            ).astype(jnp.bfloat16)
            gu_buf[my_column, c, 1, :, at] = jnp.dot(
                scaled[...], w_up[:, source], preferred_element_type=jnp.float32
            ).astype(jnp.bfloat16)
            return carry

        lax.fori_loop(0, chunk // step, gate_up, 0)
        block = gu_buf.at[my_column, c]
        gu_copies.append(spread("rep", block, block, gu_send.at[c], gu_recv.at[c]))

    for copy in sq_copies:
        copy.wait()
    total = sq_buf[0]
    for source in range(1, rep):
        total += sq_buf[source]
    scale = lax.rsqrt(total[:, :1] / D + epsilon)
    for c in range(chunks):
        for copy in gu_copies[c]:
            copy.wait()
        gate = gu_buf[0, c, 0].astype(jnp.float32)
        up = gu_buf[0, c, 1].astype(jnp.float32)
        for source in range(1, rep):
            gate += gu_buf[source, c, 0].astype(jnp.float32)
            up += gu_buf[source, c, 1].astype(jnp.float32)
        gate = gate * scale
        up = up * scale
        hidden[:, c * chunk : (c + 1) * chunk] = (gate / (1.0 + jnp.exp(-gate)) * up).astype(
            jnp.bfloat16
        )

    weights[5].wait()

    def project_down(i, carry):
        at = pl.ds(pl.multiple_of(i * tile, tile), tile)
        part = jnp.dot(hidden[...], w_down[:, at], preferred_element_type=jnp.float32).astype(
            jnp.bfloat16
        )
        for p in range(dp):
            down_send[p, :, at] = part[p * rows_here : (p + 1) * rows_here]
        return carry

    lax.fori_loop(0, width // tile, project_down, 0)
    dn_copies = [
        to("dp", peer, down_send.at[peer], down_recv.at[my_rank], dn_send.at[k], dn_recv.at[k])
        for k, peer in enumerate(ranks)
    ]
    for copy in dn_copies:
        copy.start()
    result = mixed[my_rank] + down_send[my_rank].astype(jnp.float32)
    for copy in dn_copies:
        copy.wait()
    for peer in ranks:
        result += down_recv[peer].astype(jnp.float32)
    out_ref[...] = result.astype(jnp.bfloat16)


def layer(
    query_rows,
    fresh_page,
    bias,
    residual,
    norm_gain,
    latent_store,
    up_value,
    out_proj,
    w_gate,
    w_up,
    w_down,
):
    dp, rep = lax.axis_size("dp"), lax.axis_size("rep")
    rows_here, width = residual.shape
    rows = dp * rows_here
    inner, hidden_width = out_proj.shape[0], w_gate.shape[1]
    group = dp // rep
    query_count = rep * query_rows.shape[1]
    share_rows = query_count // dp
    chunks = 3 if hidden_width % (3 * 128) == 0 else 1
    bf16, f32 = jnp.bfloat16, jnp.float32
    dma = pltpu.SemaphoreType.DMA
    vmem = pl.BlockSpec(memory_space=pltpu.VMEM)
    hbm = pl.BlockSpec(memory_space=pl.ANY)
    return pl.pallas_call(
        functools.partial(layer_kernel, dp, rep),
        out_shape=jax.ShapeDtypeStruct((rows_here, width), bf16),
        in_specs=[vmem] * 5 + [hbm] * 6,
        out_specs=vmem,
        scratch_shapes=[
            pltpu.VMEM(latent_store.shape[1:], bf16),
            pltpu.VMEM((dp,) + query_rows.shape, bf16),
            pltpu.VMEM((query_count, bias.shape[2]), f32),
            pltpu.VMEM((rep, group, query_count, CKV), bf16),
            pltpu.VMEM((rep, group, 8, query_count), f32),
            pltpu.VMEM((rep, group, query_count, CKV), bf16),
            pltpu.VMEM((rep, group, 8, query_count), f32),
            pltpu.VMEM((dp, group, share_rows, CKV), bf16),
            pltpu.VMEM((dp, group, share_rows, 128), f32),
            pltpu.VMEM((dp, group, share_rows, CKV), bf16),
            pltpu.VMEM((dp, group, share_rows, 128), f32),
            pltpu.VMEM((rep, group, rows_here, inner), bf16),
            pltpu.VMEM(up_value.shape, bf16),
            pltpu.VMEM(out_proj.shape, bf16),
            pltpu.VMEM(w_gate.shape, bf16),
            pltpu.VMEM(w_up.shape, bf16),
            pltpu.VMEM(w_down.shape, bf16),
            pltpu.VMEM((rows, inner), bf16),
            pltpu.VMEM((dp, rows_here, width), bf16),
            pltpu.VMEM((dp, rows, width), bf16),
            pltpu.VMEM((dp, rows_here, width), f32),
            pltpu.VMEM((rows, width), bf16),
            pltpu.VMEM((rep, rows, 128), f32),
            pltpu.VMEM((rep, chunks, 2, rows, hidden_width // chunks), bf16),
            pltpu.VMEM((rows, hidden_width), bf16),
            pltpu.VMEM((dp, rows_here, width), bf16),
            pltpu.VMEM((dp, rows_here, width), bf16),
            dma((6,)),
            dma((dp - 1,)),
            dma((dp - 1,)),
            dma((dp - 1, rep - 1)),
            dma((dp - 1, rep - 1)),
            dma((2, rep - 1)),
            dma((2, rep - 1)),
            dma((2, dp - 1)),
            dma((2, dp - 1)),
            dma((rep - 1,)),
            dma((rep - 1,)),
            dma((dp - 1,)),
            dma((dp - 1,)),
            dma((dp - 1,)),
            dma((dp - 1,)),
            dma((rep - 1,)),
            dma((rep - 1,)),
            dma((chunks, rep - 1)),
            dma((chunks, rep - 1)),
            dma((dp - 1,)),
            dma((dp - 1,)),
        ],
        compiler_params=pltpu.CompilerParams(
            collective_id=0, has_side_effects=True, vmem_limit_bytes=60 * 1024 * 1024
        ),
    )(
        query_rows,
        fresh_page,
        bias,
        residual,
        norm_gain.reshape(1, -1),
        latent_store,
        up_value,
        out_proj,
        w_gate,
        w_up,
        w_down,
    )


def on_device(
    latent_store,
    page_rank,
    page_index,
    lengths,
    queries,
    new_latent,
    up_value,
    out_proj,
    residual,
    norm_gain,
    w_gate,
    w_up,
    w_down,
):
    my_rank = lax.axis_index("dp")
    my_column = lax.axis_index("rep")
    rep = lax.axis_size("rep")
    rank_count, slot_count = page_rank.shape
    page_count = latent_store.shape[1]
    requests = lengths.shape[1]
    rows_here = residual.shape[0]
    steps_count = rows_here // requests
    latent_width = new_latent.shape[1]
    head_count = queries.shape[1] // latent_width
    query_rows = queries.reshape(rows_here, head_count, latent_width).transpose(1, 0, 2)
    query_rows = query_rows.reshape(rep, head_count * rows_here // rep, latent_width)
    fresh_page = jnp.pad(new_latent.T, ((0, 0), (0, PAGE - rows_here)))
    global_slot = my_column * slot_count + jnp.arange(slot_count, dtype=jnp.int32)
    row_ids = jnp.arange(rows_here, dtype=jnp.int32)
    row_request = row_ids // steps_count
    slot_counts = jnp.where(
        (global_slot // PAGES)[None, None, :] == row_request[None, :, None],
        jnp.clip(
            jnp.repeat(lengths, steps_count, axis=1)[:, :, None]
            - (global_slot % PAGES * PAGE)[None, None, :],
            0,
            PAGE,
        ),
        0,
    )
    named = (page_rank == my_rank)[:, :, None] & (
        page_index[:, :, None] == jnp.arange(page_count, dtype=jnp.int32)
    )
    limits = jnp.sum(jnp.where(named[:, None], slot_counts[..., None], 0), axis=2)
    places = jnp.arange(PAGE, dtype=jnp.int32)
    seen = places < limits[..., None]
    fresh_seen = (places[None, :] <= row_ids[:, None]) & (
        places[None, :] // steps_count == row_request[:, None]
    )
    fresh_seen = (
        fresh_seen[None]
        & (jnp.arange(rank_count) == my_rank)[:, None, None]
        & (my_column == 0)
    )
    bias = jnp.concatenate([seen, fresh_seen[:, :, None]], axis=2).astype(jnp.float32)
    bias = bias.reshape(rank_count, rows_here, -1)
    return layer(
        query_rows,
        fresh_page,
        bias,
        residual,
        norm_gain,
        latent_store,
        up_value,
        out_proj,
        w_gate,
        w_up,
        w_down,
    )


def solution(mesh):
    in_specs = (
        P(("groups", "dp"), "rep", None, None),
        P("groups", "rep"),
        P("groups", "rep"),
        P("groups", None),
        P(("groups", "dp"), None),
        P(("groups", "dp"), None),
        P("dp", None, None),
        P("dp", "rep"),
        P(("groups", "dp"), "rep"),
        P("rep"),
        P("rep", "dp"),
        P("rep", "dp"),
        P("dp", "rep"),
    )
    out_specs = P(("groups", "dp"), "rep")
    return jax.shard_map(
        on_device, mesh=mesh, in_specs=in_specs, out_specs=out_specs, check_vma=False
    )
```

time: 125 us -> 68.3 us (0.55)
  waiting for transfers between devices: 40.8 us -> 0 us
  Pallas kernels: 24.9 us -> 58.2 us
  blocking collectives: 17.4 us -> 0 us
  matrix products: 11.9 us -> 0 us
  starting transfers between devices: 9.98 us -> 0 us
  other arithmetic: 10.6 us -> 1.96 us
    all_to_all x2 -> x0, waiting for transfers between devices: 40.8 us -> none  [the longest x1 35.1 us: on_device(): lax.all_to_all(outgoing, 'dp', split_axis=0, concat_axis=0, tiled=True)]
    pallas_call x1, Pallas kernels: 24.9 us -> 58.2 us  [layer(): pl.pallas_call(functools.partial(layer_kernel, dp, rep), out_shape=jax.Sh...]
    all_gather x3 -> x0, blocking collectives: 17.4 us -> none  [merged_2(): lax.all_gather(a.astype(kind), axis)]
    dot_general x5 -> x0, matrix products: 11.9 us -> none  [the longest x1 7.4 us: join_pages(): jnp.einsum('jpsh,pshc->jshc', factor, partial_value, precision=lax.Precis...]
    all_to_all x2 -> x0, starting transfers between devices: 9.98 us -> none  [the longest x1 6.48 us: on_device(): lax.all_to_all(outgoing, 'dp', split_axis=0, concat_axis=0, tiled=True)]
    gather x3 -> x0, local copies, waits for them, and re-layouts: 4.7 us -> none  [the longest x1 2.05 us: on_device(): restored = jnp.take(arrived, arrival_slot, axis=0)]
    reshape x2 -> x4, local copies, waits for them, and re-layouts: 0.69 us -> 3.35 us  [the longest x1 1.29 us: layer(): norm_gain.reshape(1, -1)]
    select_n x3 -> x4, other arithmetic: 3.24 us -> 0.75 us  [the longest x1 0.73 us: on_device(): jnp.where((global_slot // PAGES)[None, None, :] == row_request[None, :, N...]
  transfers between devices with their start and end apart: 2 -> 0, of which waited for: 2 -> 0; matrix products, arithmetic and copies ran while one was open for 5% -> 0% of each run, Pallas kernels for 0% -> 0%
where the time goes in v2:
time: 68.3 us; the launch traced here: 67.9 us
  Pallas kernels  58.2 us (85%)
  local copies, waits for them, and re-layouts  7.74 us (11%)
  other arithmetic  1.96 us (3%)
    pallas_call x1, Pallas kernels, layer(): pl.pallas_call(functools.partial(layer_kernel, dp, rep), out_shape=jax.Sh...  58.2 us
    unnamed x3, local copies, waits for them, and re-layouts  2.93 us

profile of v2, /device:TPU:0, one launch (start us, length us, event | category | flops | bytes accessed | tf_op | source)
XLA Modules:
  0.0 67.9 jit_solution(11452172226828347452)
XLA Ops:
  0.0 1.1 %reshape.188 = bf16[2,64,576]{2,1,0:T(8,128)(2,1)S(1)} reshape(bf16[2,36864]{1,0:T(2,128)(2,1)} %param.17) | data formatting | bytes 294912 | tf_op jit(solution)/shard_map/reshape | solution.py:499
  1.1 0.2 copy.24
  1.3 0.8 %reshape.189.query_ref = bf16[4,32,576]{2,1,0:T(8,128)(2,1)} reshape(bf16[64,2,576]{2,1,0:T(2,128)(2,1)S(1)} %bitcast.5) | data formatting | bytes 294912 | tf_op jit(solution)/shard_map/reshape | solution.py:500
  2.1 0.9 %copy.19 = bf16[2,576]{0,1:T(8,128)(2,1)S(1)} copy(bf16[2,576]{1,0:T(2,128)(2,1)} %param.18) | data formatting | bytes 4608 | tf_op args[5]
  2.9 0.7 %pad.4.fresh_ref = bf16[576,128]{1,0:T(8,128)(2,1)} pad(bf16[576,2]{1,0:T(8,128)(2,1)S(1)} %bitcast.6, bf16[]{:T(256)} %constant.52.clone.1), padding=0_0x0_126 | pad | bytes 149762 | tf_op jit(solution)/shard_map/jit(_pad)/pad | solution.py:501
  3.6 0.1 compare_and_fusion
  3.7 0.1 and_and_fusion
  3.8 0.1 broadcast_compare_fusion.1
  3.9 0.7 %clamp_select_fusion = s32[4,2,12]{0,2,1:T(8,128)S(1)} fusion(s32[12]{0:T(128)S(1)} %get-tuple-element.6, s32[4]{0:T(128)} %bitcast.7, pred[2,12]{1,0:T(4,128)(4,1)S(1)} %broadcast_compare_fusion.1), kind=kLoop, calls=%fused_computation.6 | loop fusion | flops 288 | bytes 472 | tf_op jit(solution)/shard_map/jit(_where)/select_n | solution.py:505
  4.6 0.8 %copy.21 = s32[4,12]{0,1:T(8,128)S(1)} copy(s32[4,12]{1,0:T(4,128)} %param.15) | data formatting | bytes 384 | tf_op args[2]
  5.4 0.7 %broadcast_compare_fusion = pred[4,12]{1,0:T(4,128)(4,1)S(1)} fusion(s32[4,12]{1,0:T(4,128)} %param.14, s32[]{:T(128)S(6)} %axis_index.23), kind=kLoop, calls=%fused_computation.19 | loop fusion | flops 48 | bytes 244 | tf_op jit(solution)/shard_map/eq | solution.py:515
  6.1 0.1 copy.20
  6.2 0.1 fusion
  6.3 0.1 select_reduce_fusion
  6.4 0.1 iota_compare_fusion
  6.5 0.7 reshape.191.bias_ref
  7.2 1.3 %reshape.190.gain_ref = f32[1,1792]{1,0:T(1,128)} reshape(f32[1792]{0:T(1024)} %param.22) | data formatting | bytes 14336 | tf_op jit(solution)/shard_map/reshape | solution.py:464
  8.4 58.2 %shard_map.130 = bf16[2,1792]{1,0:T(2,128)(2,1)} custom-call(bf16[4,32,576]{2,1,0:T(8,128)(2,1)} %reshape.189.query_ref, bf16[576,128]{1,0:T(8,128)(2,1)} %pad.4.fresh_ref, f32[4,2,1664]{2,1,0:T(2,128)} %reshape.191.bias_ref, bf16[2,1792]{1,0:T(2,128)(2,1)} %residual_ref.1, f32[1,1792]{1,0:T(1,128)} %reshape.190.gain_ref, ...), custom_call_target="tpu_custom_call" | custom-call | tf_op jit(solution)/shard_map/pallas_call | solution.py:401
  66.7 1.3 %copy.26 = bf16[2,1792]{1,0:T(2,128)(2,1)} copy(bf16[2,1792]{1,0:T(2,128)(2,1)} %shard_map.130) | data formatting | bytes 14336
  (6 shorter events, 0.0 us)
